TPU v7x, 32 devices: a whole 2x2x4 slice. The times are simulated.
32 devices in a mesh: col: 8 (over y, x, core), grp: 4 (over z).
Axes of the slice: x: 2, y: 2, z: 4, core: 2. Of those that a mesh axis runs over, the one named last changes fastest.
Arguments:
- profiles: float32 [2048, 116], P('col'), may hold values from -6 to 6
- courant: float32 [2048, 58], P('col'), may hold values from -0.7 to 0.7
- owner_map: int32 [2048], replicated, may hold values from 0 to 2047, as said below
- cloud_flags: int32 [2048], P('col'), may hold values 0 or 1
- crm_state: float32 [2, 58, 64, 2048], P(None, None, 'grp', 'col'), may hold values from -6 to 6
Outputs:
- tendency: float32 [2048, 116], P('col')
- crm_final: float32 [2, 58, 64, 2048], P(None, None, 'grp', 'col')
Inputs may be any that keep to these rules, and one draw needn't show every extreme that they name: owner_map is a permutation; physics column p lives in span p // 256, element column e in group e // 256; each group hands at most 34 columns to one span, and exactly 34 to some spans, and every span receives exactly 256 columns.
All inputs are finite; a program needn't handle non-finite values. No bound on the sum of `cloud_flags` on one device may be relied on, other than what follows from the above.
Results may differ from a plain program's by a relative error of at most 0.00002.
Values sent between devices are 32-bit elements; how exact they have to be, the bound alone decides.
A program may use at most 64 MiB of HBM per device.

v0:
```python
import jax
import jax.numpy as jnp
from jax import lax
from jax.sharding import PartitionSpec as P

STEPS = 8
diffuse_x = 0.25
diffuse_z = 0.2
sat_scale = 0.5
sat_slope = 0.3
cond_rate = 0.5
latent_gain = 0.4


def padded(x, sides, width):
    for axis, dim in sides:
        peers, length = (lax.axis_size(axis), x.shape[dim])
        up = [(i, (i + 1) % peers) for i in range(peers)]
        down = [(j, i) for i, j in up]
        last = lax.slice_in_dim(x, length - width, length, axis=dim)
        leading = lax.slice_in_dim(x, 0, width, axis=dim)
        before = lax.ppermute(last, axis, up)
        after = lax.ppermute(leading, axis, down)
        x = jnp.concatenate([before, x, after], axis=dim)
    return x


def condense(fields, cloudy):
    energy = fields[0]
    moisture = fields[1]
    saturation = sat_scale * (jnp.exp(sat_slope * energy) - 1.0)
    amount = cond_rate * jnp.maximum(moisture - saturation, 0.0) * cloudy
    return jnp.stack([energy + latent_gain * amount, moisture - amount])


def advance(widened, courant_here, forcing, cloudy):
    centre = widened[:, :, 1:-1]
    eastern = widened[:, :, 2:]
    western = widened[:, :, :-2]
    upper = jnp.concatenate([centre[:, 1:], centre[:, -1:]], axis=1)
    lower = jnp.concatenate([centre[:, :1], centre[:, :-1]], axis=1)
    stepped = (
        centre
        + courant_here * ((western - eastern) * 0.5)
        + diffuse_x * (eastern - 2.0 * centre + western)
        + diffuse_z * (upper - 2.0 * centre + lower)
        + forcing
    )
    return condense(stepped, cloudy)


def on_device(profiles, courant, owner_map, cloud_flags, crm_state):
    columns = profiles.shape[0]
    levels = courant.shape[1]
    col_count = lax.axis_size("col")
    col_index = lax.axis_index("col")
    per_peer = columns // col_count
    capacity = per_peer + min(2, per_peer)
    positions = jnp.arange(columns, dtype=jnp.int32)
    my_owner = lax.dynamic_slice_in_dim(owner_map, col_index * columns, columns)
    target = my_owner // columns
    earlier = (target[:, None] == target[None, :]) & (positions[None, :] < positions[:, None])
    order_in = jnp.sum(earlier.astype(jnp.int32), axis=1)
    sent_slot = target * capacity + order_in
    send_rows = jnp.full((col_count * capacity,), columns, jnp.int32).at[sent_slot].set(positions)
    padded_prof = jnp.concatenate([profiles, jnp.zeros((1, profiles.shape[1]), jnp.float32)])
    padded_cour = jnp.concatenate([courant, jnp.zeros((1, levels), jnp.float32)])
    out_prof = padded_prof[send_rows].reshape(col_count, capacity, profiles.shape[1])
    out_cour = padded_cour[send_rows].reshape(col_count, capacity, levels)
    got_prof, got_cour = (
        lax.all_to_all(out_prof, "col", split_axis=0, concat_axis=0, tiled=True),
        lax.all_to_all(out_cour, "col", split_axis=0, concat_axis=0, tiled=True),
    )
    block_view = owner_map.reshape(col_count, columns)
    landing = (block_view // columns == col_index).astype(jnp.int32)
    before = jnp.cumsum(landing, axis=1) - landing
    sources = jnp.arange(col_count, dtype=jnp.int32)[:, None]
    where_from = sources * capacity + before
    landing_slot = jnp.where(landing > 0, block_view - col_index * columns, columns)
    senders_block = 4
    slot_blocks = landing_slot.reshape(col_count // senders_block, senders_block * columns)
    from_blocks = where_from.reshape(col_count // senders_block, senders_block * columns)

    def match_block(found, pair):
        slots, anchors = pair
        hits = slots[None, :] == positions[:, None]
        return (found + jnp.sum(jnp.where(hits, anchors[None, :], 0), axis=1), None)

    take_rows, unused = lax.scan(
        match_block, jnp.zeros((columns,), jnp.int32), (slot_blocks, from_blocks)
    )
    phys_prof = got_prof.reshape(col_count * capacity, profiles.shape[1])[take_rows]
    phys_cour = got_cour.reshape(col_count * capacity, levels)[take_rows]
    forcing = (phys_prof.reshape(columns, 2, levels).transpose(1, 2, 0) / STEPS)[:, :, None, :]
    courant_here = phys_cour.T[None, :, None, :]
    cloudy = cloud_flags.astype(jnp.float32)
    crm_now = crm_state
    for repeat in range(STEPS // 2):
        widened = padded(crm_now, (("grp", 2),), 2)
        middle = advance(widened, courant_here, forcing, cloudy)
        crm_now = advance(middle, courant_here, forcing, cloudy)
    cells_all = crm_state.shape[2] * lax.axis_size("grp")
    partial_value = jnp.sum(crm_now, axis=2) - jnp.sum(crm_state, axis=2)
    totals = lax.psum(partial_value, "grp")
    increment = totals / cells_all
    phys_inc = increment.transpose(2, 0, 1).reshape(columns, 2 * levels)
    back_rows = (
        jnp.zeros((col_count * capacity, 2 * levels), jnp.float32).at[take_rows].set(phys_inc)
    )
    got_back = lax.all_to_all(
        back_rows.reshape(col_count, capacity, 2 * levels),
        "col",
        split_axis=0,
        concat_axis=0,
        tiled=True,
    )
    tendency = got_back.reshape(col_count * capacity, 2 * levels)[sent_slot]
    return (tendency, crm_now)


def solution(mesh):
    placed = (P("col", None), P("col", None), P(), P("col"), P(None, None, "grp", "col"))
    return jax.shard_map(
        on_device,
        mesh=mesh,
        in_specs=placed,
        out_specs=(P("col", None), P(None, None, "grp", "col")),
        check_vma=False,
    )
```

profile of v0, /device:TPU:0, one launch (start us, length us, event | category | flops | bytes accessed | tf_op | source)
XLA Modules:
  0.0 158.9 jit_solution(1841023109057067718)
XLA Ops:
  7.2 0.9 and_select_fusion.1
  8.3 0.8 compare_select_fusion.2
  9.1 1.4 scatter_custom_fusion
  10.5 0.9 copy.71
  11.5 1.1 gather_fusion
  12.6 0.9 reshape.148
  13.4 5.2 %all-to-all-start = ((f32[8,1,1972]{2,1,0:T(1,128)}), f32[8,1,1972]{2,1,0:T(1,128)S(1)}, u32[]{:S(2)}, u32[]{:S(2)}) async-start(f32[8,1,1972]{2,1,0:T(1,128)} %reshape.148), calls=%async_computation | async-start | bytes 131072 | tf_op jit(solution)/shard_map/all_to_all | solution.py:72
  18.8 1.6 %collective-permute-start = (f32[2,58,2,256]{3,1,2,0:T(8,128)S(1)}, f32[2,58,2,256]{3,1,2,0:T(8,128)S(1)}, u32[]{:S(2)}, u32[]{:S(2)}) collective-permute-start(f32[2,58,2,256]{3,1,2,0:T(8,128)S(1)} %copy.84), channel_id=1, source_target_pairs={{0,1},{1,2},{2,3},{3,0},{4,5},{5,6},{6,7},{7,4},{8,9},{9,10},{10,1... | collective-permute-start | bytes 712712 | tf_op jit(solution)/shard_map/ppermute | solution.py:22
  20.5 2.3 %collective-permute-start.1 = (f32[2,58,2,256]{3,1,2,0:T(8,128)S(1)}, f32[2,58,2,256]{3,1,2,0:T(8,128)S(1)}, u32[]{:S(2)}, u32[]{:S(2)}) collective-permute-start(f32[2,58,2,256]{3,1,2,0:T(8,128)S(1)} %copy.85), channel_id=1, source_target_pairs={{1,0},{2,1},{3,2},{0,3},{5,4},{6,5},{7,6},{4,7},{9,8},{10,9},{11,1... | collective-permute-start | bytes 712712 | tf_op jit(solution)/shard_map/ppermute | solution.py:23
  22.8 0.6 reduce-window.6
  23.9 0.5 while.11
  24.6 1.1 gather_fusion.2
  25.6 0.7 reshape.75
  26.3 4.2 %all-to-all-start.1 = ((f32[8,34,116]{2,1,0:T(8,128)}), f32[8,34,116]{2,1,0:T(8,128)S(1)}, u32[]{:S(2)}, u32[]{:S(2)}) async-start(f32[8,34,116]{2,1,0:T(8,128)} %reshape.75), calls=%async_computation.1 | async-start | bytes 327680 | tf_op jit(solution)/shard_map/all_to_all | solution.py:71
  30.6 0.5 broadcast.477
  31.1 0.8 reduce.2
  32.0 0.7 gather_fusion.1
  32.9 3.5 %all-to-all-done.1 = f32[8,34,116]{2,1,0:T(8,128)S(1)} async-done(((f32[8,34,116]{2,1,0:T(8,128)}), f32[8,34,116]{2,1,0:T(8,128)S(1)}, u32[]{:S(2)}, u32[]{:S(2)}) %all-to-all-start.1) | async-done | bytes 126240 | tf_op jit(solution)/shard_map/all_to_all | solution.py:71
  36.4 0.7 gather_fusion.3
  37.3 1.3 constant_dynamic-update-slice_fusion.6
  38.7 0.6 fusion.111
  39.4 1.8 %fusion.44 = f32[2,58,18,256]{3,1,2,0:T(8,128)S(1)} fusion(f32[2,1,18,256]{3,1,2,0:T(1,128)S(1)} %get-tuple-element.78, f32[2,57,18,256]{3,1,2,0:T(8,128)S(1)} %get-tuple-element.80, f32[2,57,18,256]{3,1,2,0:T(8,128)S(1)} %get-tuple-element.79, f32[2,1,18,256]{3,1,2,0:T(1,128)S(1)} %get-tuple-element.77, f32[2,58,18,256]{3,1,2,0:T(8,128)S(1)} %get-tuple-element.115, ...), kind=kLoop, calls=%fused_computation.133 | loop fusion | flops 8017920 | bytes 13006848 | tf_op jit(solution)/shard_map/add | solution.py:43
  41.2 0.5 multiply_add_fusion.3
  42.0 1.7 %fusion.80 = f32[2,58,16,256]{3,1,2,0:T(8,128)S(1)} fusion(f32[1,58,18,256]{3,1,2,0:T(8,128)S(1)} %get-tuple-element.88, f32[1,58,18,256]{3,1,2,0:T(8,128)S(1)} %get-tuple-element.87, f32[2,1,16,256]{3,1,2,0:T(1,128)S(1)} %get-tuple-element.96, f32[2,57,16,256]{3,1,2,0:T(8,128)S(1)} %fusion.60, f32[2,1,16,256]{3,1,2,0:T(1,128)S(1)} %get-tuple-element.95, ...), kind=kLoop, calls=%fused_computation.179 | loop fusion | flops 9027584 | bytes 6150144 | tf_op jit(solution)/shard_map/add | solution.py:43
  43.7 0.5 fusion.88
  44.3 3.8 %collective-permute-start.3 = (f32[2,58,2,256]{3,1,2,0:T(8,128)S(1)}, f32[2,58,2,256]{3,1,2,0:T(8,128)S(1)}, u32[]{:S(2)}, u32[]{:S(2)}) collective-permute-start(f32[2,58,2,256]{3,1,2,0:T(8,128)S(1)} %get-tuple-element.111), channel_id=1, source_target_pairs={{1,0},{2,1},{3,2},{0,3},{5,4},{6,5},{7,6},{4,7},{9,8},{10,9},{11,1... | collective-permute-start | bytes 712712 | tf_op jit(solution)/shard_map/ppermute | solution.py:23
  48.1 7.2 %collective-permute-done.2 = f32[2,58,2,256]{3,1,2,0:T(8,128)S(1)} collective-permute-done((f32[2,58,2,256]{3,1,2,0:T(8,128)S(1)}, f32[2,58,2,256]{3,1,2,0:T(8,128)S(1)}, u32[]{:S(2)}, u32[]{:S(2)}) %collective-permute-start.2) | collective-permute-done | bytes 237600 | tf_op jit(solution)/shard_map/ppermute | solution.py:22
  55.2 2.6 %collective-permute-done.3 = f32[2,58,2,256]{3,1,2,0:T(8,128)S(1)} collective-permute-done((f32[2,58,2,256]{3,1,2,0:T(8,128)S(1)}, f32[2,58,2,256]{3,1,2,0:T(8,128)S(1)}, u32[]{:S(2)}, u32[]{:S(2)}) %collective-permute-start.3) | collective-permute-done | bytes 237600 | tf_op jit(solution)/shard_map/ppermute | solution.py:23
  57.9 0.3 pad_maximum_fusion
  58.1 0.6 fusion.109
  58.8 2.2 %fusion.10 = f32[2,58,18,256]{3,1,2,0:T(8,128)S(1)} fusion(f32[1,58,16,256]{3,1,2,0:T(8,128)S(1)} %get-tuple-element.104, f32[1,58,16,256]{3,1,2,0:T(8,128)S(1)} %get-tuple-element.103, f32[2,58,2,256]{3,1,2,0:T(8,128)S(1)} %collective-permute-done.2, f32[2,58,2,256]{3,1,2,0:T(8,128)S(1)} %collective-permute-done.3, ...), kind=kLoop, calls=%fused_computation.96 | loop fusion | flops 18708480 | bytes 11032576 | tf_op jit(solution)/shard_map/add | solution.py:43
  60.9 0.5 multiply_add_fusion.2
  61.7 1.7 %fusion.75 = f32[2,58,16,256]{3,1,2,0:T(8,128)S(1)} fusion(f32[1,58,18,256]{3,1,2,0:T(8,128)S(1)} %get-tuple-element.86, f32[1,58,18,256]{3,1,2,0:T(8,128)S(1)} %get-tuple-element.85, f32[2,1,16,256]{3,1,2,0:T(1,128)S(1)} %get-tuple-element.94, f32[2,57,16,256]{3,1,2,0:T(8,128)S(1)} %fusion.56, f32[2,1,16,256]{3,1,2,0:T(1,128)S(1)} %get-tuple-element.93, ...), kind=kLoop, calls=%fused_computation.173 | loop fusion | flops 9027584 | bytes 6150144 | tf_op jit(solution)/shard_map/add | solution.py:43
  63.4 0.5 fusion.87
  63.9 0.9 collective-permute-start.4
  64.8 3.0 %collective-permute-start.5 = (f32[2,58,2,256]{3,1,2,0:T(8,128)S(1)}, f32[2,58,2,256]{3,1,2,0:T(8,128)S(1)}, u32[]{:S(2)}, u32[]{:S(2)}) collective-permute-start(f32[2,58,2,256]{3,1,2,0:T(8,128)S(1)} %get-tuple-element.109), channel_id=1, source_target_pairs={{1,0},{2,1},{3,2},{0,3},{5,4},{6,5},{7,6},{4,7},{9,8},{10,9},{11,1... | collective-permute-start | bytes 712712 | tf_op jit(solution)/shard_map/ppermute | solution.py:23
  67.8 7.2 %collective-permute-done.4 = f32[2,58,2,256]{3,1,2,0:T(8,128)S(1)} collective-permute-done((f32[2,58,2,256]{3,1,2,0:T(8,128)S(1)}, f32[2,58,2,256]{3,1,2,0:T(8,128)S(1)}, u32[]{:S(2)}, u32[]{:S(2)}) %collective-permute-start.4) | collective-permute-done | bytes 237600 | tf_op jit(solution)/shard_map/ppermute | solution.py:22
  75.0 2.3 %collective-permute-done.5 = f32[2,58,2,256]{3,1,2,0:T(8,128)S(1)} collective-permute-done((f32[2,58,2,256]{3,1,2,0:T(8,128)S(1)}, f32[2,58,2,256]{3,1,2,0:T(8,128)S(1)}, u32[]{:S(2)}, u32[]{:S(2)}) %collective-permute-start.5) | collective-permute-done | bytes 237600 | tf_op jit(solution)/shard_map/ppermute | solution.py:23
  77.2 0.3 pad_maximum_fusion.1
  77.5 0.6 fusion.108
  78.2 2.2 %fusion.23 = f32[2,58,18,256]{3,1,2,0:T(8,128)S(1)} fusion(f32[1,58,16,256]{3,1,2,0:T(8,128)S(1)} %get-tuple-element.102, f32[1,58,16,256]{3,1,2,0:T(8,128)S(1)} %get-tuple-element.101, f32[2,58,2,256]{3,1,2,0:T(8,128)S(1)} %collective-permute-done.4, f32[2,58,2,256]{3,1,2,0:T(8,128)S(1)} %collective-permute-done.5, ...), kind=kLoop, calls=%fused_computation.109 | loop fusion | flops 18708480 | bytes 11032576 | tf_op jit(solution)/shard_map/add | solution.py:43
  80.3 0.5 multiply_add_fusion.1
  81.1 1.7 %fusion.70 = f32[2,58,16,256]{3,1,2,0:T(8,128)S(1)} fusion(f32[1,58,18,256]{3,1,2,0:T(8,128)S(1)} %get-tuple-element.84, f32[1,58,18,256]{3,1,2,0:T(8,128)S(1)} %get-tuple-element.83, f32[2,1,16,256]{3,1,2,0:T(1,128)S(1)} %get-tuple-element.92, f32[2,57,16,256]{3,1,2,0:T(8,128)S(1)} %fusion.52, f32[2,1,16,256]{3,1,2,0:T(1,128)S(1)} %get-tuple-element.91, ...), kind=kLoop, calls=%fused_computation.167 | loop fusion | flops 9027584 | bytes 6150144 | tf_op jit(solution)/shard_map/add | solution.py:43
  82.8 0.4 fusion.86
  83.2 1.7 %collective-permute-start.6 = (f32[2,58,2,256]{3,1,2,0:T(8,128)S(1)}, f32[2,58,2,256]{3,1,2,0:T(8,128)S(1)}, u32[]{:S(2)}, u32[]{:S(2)}) collective-permute-start(f32[2,58,2,256]{3,1,2,0:T(8,128)S(1)} %get-tuple-element.108), channel_id=1, source_target_pairs={{0,1},{1,2},{2,3},{3,0},{4,5},{5,6},{6,7},{7,4},{8,9},{9,10},{10,1... | collective-permute-start | bytes 712712 | tf_op jit(solution)/shard_map/ppermute | solution.py:22
  84.9 2.2 %collective-permute-start.7 = (f32[2,58,2,256]{3,1,2,0:T(8,128)S(1)}, f32[2,58,2,256]{3,1,2,0:T(8,128)S(1)}, u32[]{:S(2)}, u32[]{:S(2)}) collective-permute-start(f32[2,58,2,256]{3,1,2,0:T(8,128)S(1)} %get-tuple-element.107), channel_id=1, source_target_pairs={{1,0},{2,1},{3,2},{0,3},{5,4},{6,5},{7,6},{4,7},{9,8},{10,9},{11,1... | collective-permute-start | bytes 712712 | tf_op jit(solution)/shard_map/ppermute | solution.py:23
  87.1 1.9 %reduce_sum.38 = f32[2,58,256]{2,1,0:T(8,128)S(1)} reduce(f32[2,58,16,256]{3,2,1,0:T(8,128)} %param.11, f32[]{:T(128)} %constant.35.clone.1), dimensions={2}, to_apply=%region_8.9 | reduce | flops 445440 | bytes 2019332 | tf_op jit(solution)/shard_map/reduce_sum | solution.py:103
  89.0 5.3 %collective-permute-done.6 = f32[2,58,2,256]{3,1,2,0:T(8,128)S(1)} collective-permute-done((f32[2,58,2,256]{3,1,2,0:T(8,128)S(1)}, f32[2,58,2,256]{3,1,2,0:T(8,128)S(1)}, u32[]{:S(2)}, u32[]{:S(2)}) %collective-permute-start.6) | collective-permute-done | bytes 237600 | tf_op jit(solution)/shard_map/ppermute | solution.py:22
  94.3 3.6 %collective-permute-done.7 = f32[2,58,2,256]{3,1,2,0:T(8,128)S(1)} collective-permute-done((f32[2,58,2,256]{3,1,2,0:T(8,128)S(1)}, f32[2,58,2,256]{3,1,2,0:T(8,128)S(1)}, u32[]{:S(2)}, u32[]{:S(2)}) %collective-permute-start.7) | collective-permute-done | bytes 237600 | tf_op jit(solution)/shard_map/ppermute | solution.py:23
  98.1 0.6 fusion.107
  98.7 2.0 %fusion.36 = f32[2,58,18,256]{3,1,2,0:T(8,128)S(1)} fusion(f32[1,58,16,256]{3,1,2,0:T(8,128)S(1)} %get-tuple-element.100, f32[1,58,16,256]{3,1,2,0:T(8,128)S(1)} %get-tuple-element.99, f32[2,58,2,256]{3,1,2,0:T(8,128)S(1)} %collective-permute-done.6, f32[2,58,2,256]{3,1,2,0:T(8,128)S(1)} %collective-permute-done.7, ...), kind=kLoop, calls=%fused_computation.122 | loop fusion | flops 18708480 | bytes 11032576 | tf_op jit(solution)/shard_map/add | solution.py:43
  100.8 0.5 multiply_add_fusion
  101.5 1.7 %fusion.65 = f32[2,58,16,256]{3,1,2,0:T(8,128)S(1)} fusion(f32[1,58,18,256]{3,1,2,0:T(8,128)S(1)} %get-tuple-element.82, f32[1,58,18,256]{3,1,2,0:T(8,128)S(1)} %get-tuple-element.81, f32[2,1,16,256]{3,1,2,0:T(1,128)S(1)} %get-tuple-element.90, f32[2,57,16,256]{3,1,2,0:T(8,128)S(1)} %fusion.48, f32[2,1,16,256]{3,1,2,0:T(1,128)S(1)} %get-tuple-element.89, ...), kind=kLoop, calls=%fused_computation.161 | loop fusion | flops 9027584 | bytes 6150144 | tf_op jit(solution)/shard_map/add | solution.py:43
  103.2 0.4 multiply_add_fusion.4
  103.8 0.7 sub.250
  104.5 33.6 %all-reduce.4.cloned.1.call-done = f32[2,58,256]{2,1,0:T(8,128)} async-done(((f32[2,58,256]{2,1,0:T(8,128)}), f32[2,58,256]{2,1,0:T(8,128)}) %all-reduce.4.cloned.1.call-update) | async-done | bytes 118800 | tf_op jit(solution)/shard_map/psum | solution.py:104
  138.1 0.9 multiply_bitcast_fusion
  139.2 1.2 scatter_custom_fusion.1
  140.3 0.7 reshape.78
  141.0 3.6 %all-to-all-start.2 = ((f32[8,34,116]{2,1,0:T(8,128)}), f32[8,34,116]{2,1,0:T(8,128)S(1)}, u32[]{:S(2)}, u32[]{:S(2)}) async-start(f32[8,34,116]{2,1,0:T(8,128)} %reshape.78), calls=%async_computation.2 | async-start | bytes 327680 | tf_op jit(solution)/shard_map/all_to_all | solution.py:110
  144.7 2.4 %copy.78 = f32[2,58,16,256]{3,2,1,0:T(8,128)} copy(f32[2,58,16,256]{3,1,2,0:T(8,128)S(1)} %get-tuple-element.105) | data formatting | bytes 3801088
  147.0 3.5 %all-to-all-done.2 = f32[8,34,116]{2,1,0:T(8,128)S(1)} async-done(((f32[8,34,116]{2,1,0:T(8,128)}), f32[8,34,116]{2,1,0:T(8,128)S(1)}, u32[]{:S(2)}, u32[]{:S(2)}) %all-to-all-start.2) | async-done | bytes 126240 | tf_op jit(solution)/shard_map/all_to_all | solution.py:110
  150.5 0.7 gather_fusion.4
  151.3 0.8 copy.77
  (76 shorter events, 3.9 us)
Async XLA Ops:
  7.2 15.6 %copy-start.2 = (s32[2048]{0:T(1024)S(1)}, s32[2048]{0:T(1024)}, u32[]{:S(2)}) copy-start(s32[2048]{0:T(1024)} %param.9) | copy-start | bytes 24580
  7.2 11.4 %copy-start = (f32[2,58,16,256]{3,2,1,0:T(8,128)S(1)}, f32[2,58,16,256]{3,2,1,0:T(8,128)}, u32[]{:S(2)}) copy-start(f32[2,58,16,256]{3,2,1,0:T(8,128)} %param.11) | copy-start | bytes 5701636
  11.4 13.0 %copy-start.3 = (s32[256]{0:T(256)S(1)}, s32[256]{0:T(256)}, u32[]{:S(2)}) copy-start(s32[256]{0:T(256)} %param.10) | copy-start | bytes 3076
  11.4 13.0 %copy-start.1 = (f32[256,116]{0,1:T(8,128)S(1)}, f32[256,116]{0,1:T(8,128)}, u32[]{:S(2)}) copy-start(f32[256,116]{0,1:T(8,128)} %param.7) | copy-start | bytes 356356
  13.4 12.9 %all-to-all-start = ((f32[8,1,1972]{2,1,0:T(1,128)}), f32[8,1,1972]{2,1,0:T(1,128)S(1)}, u32[]{:S(2)}, u32[]{:S(2)}) async-start(f32[8,1,1972]{2,1,0:T(1,128)} %reshape.148), calls=%async_computation | async-start | bytes 131072 | tf_op jit(solution)/shard_map/all_to_all | solution.py:72
  18.8 18.4 %collective-permute-start = (f32[2,58,2,256]{3,1,2,0:T(8,128)S(1)}, f32[2,58,2,256]{3,1,2,0:T(8,128)S(1)}, u32[]{:S(2)}, u32[]{:S(2)}) collective-permute-start(f32[2,58,2,256]{3,1,2,0:T(8,128)S(1)} %copy.84), channel_id=1, source_target_pairs={{0,1},{1,2},{2,3},{3,0},{4,5},{5,6},{6,7},{7,4},{8,9},{9,10},{10,1... | collective-permute-start | bytes 712712 | tf_op jit(solution)/shard_map/ppermute | solution.py:22
  20.5 18.2 %collective-permute-start.1 = (f32[2,58,2,256]{3,1,2,0:T(8,128)S(1)}, f32[2,58,2,256]{3,1,2,0:T(8,128)S(1)}, u32[]{:S(2)}, u32[]{:S(2)}) collective-permute-start(f32[2,58,2,256]{3,1,2,0:T(8,128)S(1)} %copy.85), channel_id=1, source_target_pairs={{1,0},{2,1},{3,2},{0,3},{5,4},{6,5},{7,6},{4,7},{9,8},{10,9},{11,1... | collective-permute-start | bytes 712712 | tf_op jit(solution)/shard_map/ppermute | solution.py:23
  26.3 10.0 %all-to-all-start.1 = ((f32[8,34,116]{2,1,0:T(8,128)}), f32[8,34,116]{2,1,0:T(8,128)S(1)}, u32[]{:S(2)}, u32[]{:S(2)}) async-start(f32[8,34,116]{2,1,0:T(8,128)} %reshape.75), calls=%async_computation.1 | async-start | bytes 327680 | tf_op jit(solution)/shard_map/all_to_all | solution.py:71
  30.5 107.6 %all-reduce.4.cloned.1.call-start = ((), (), s32[]{:S(2)}) async-start(), calls=%async_computation.3 | async-start | bytes 262144 | tf_op jit(solution)/shard_map/psum | solution.py:104
  44.2 11.0 %collective-permute-start.2 = (f32[2,58,2,256]{3,1,2,0:T(8,128)S(1)}, f32[2,58,2,256]{3,1,2,0:T(8,128)S(1)}, u32[]{:S(2)}, u32[]{:S(2)}) collective-permute-start(f32[2,58,2,256]{3,1,2,0:T(8,128)S(1)} %get-tuple-element.112), channel_id=1, source_target_pairs={{0,1},{1,2},{2,3},{3,0},{4,5},{5,6},{6,7},{7,4},{8,9},{9,10},{10,1... | collective-permute-start | bytes 712712 | tf_op jit(solution)/shard_map/ppermute | solution.py:22
  44.3 13.6 %collective-permute-start.3 = (f32[2,58,2,256]{3,1,2,0:T(8,128)S(1)}, f32[2,58,2,256]{3,1,2,0:T(8,128)S(1)}, u32[]{:S(2)}, u32[]{:S(2)}) collective-permute-start(f32[2,58,2,256]{3,1,2,0:T(8,128)S(1)} %get-tuple-element.111), channel_id=1, source_target_pairs={{1,0},{2,1},{3,2},{0,3},{5,4},{6,5},{7,6},{4,7},{9,8},{10,9},{11,1... | collective-permute-start | bytes 712712 | tf_op jit(solution)/shard_map/ppermute | solution.py:23
  63.9 11.0 %collective-permute-start.4 = (f32[2,58,2,256]{3,1,2,0:T(8,128)S(1)}, f32[2,58,2,256]{3,1,2,0:T(8,128)S(1)}, u32[]{:S(2)}, u32[]{:S(2)}) collective-permute-start(f32[2,58,2,256]{3,1,2,0:T(8,128)S(1)} %get-tuple-element.110), channel_id=1, source_target_pairs={{0,1},{1,2},{2,3},{3,0},{4,5},{5,6},{6,7},{7,4},{8,9},{9,10},{10,1... | collective-permute-start | bytes 712712 | tf_op jit(solution)/shard_map/ppermute | solution.py:22
  64.8 12.4 %collective-permute-start.5 = (f32[2,58,2,256]{3,1,2,0:T(8,128)S(1)}, f32[2,58,2,256]{3,1,2,0:T(8,128)S(1)}, u32[]{:S(2)}, u32[]{:S(2)}) collective-permute-start(f32[2,58,2,256]{3,1,2,0:T(8,128)S(1)} %get-tuple-element.109), channel_id=1, source_target_pairs={{1,0},{2,1},{3,2},{0,3},{5,4},{6,5},{7,6},{4,7},{9,8},{10,9},{11,1... | collective-permute-start | bytes 712712 | tf_op jit(solution)/shard_map/ppermute | solution.py:23
  83.2 11.1 %collective-permute-start.6 = (f32[2,58,2,256]{3,1,2,0:T(8,128)S(1)}, f32[2,58,2,256]{3,1,2,0:T(8,128)S(1)}, u32[]{:S(2)}, u32[]{:S(2)}) collective-permute-start(f32[2,58,2,256]{3,1,2,0:T(8,128)S(1)} %get-tuple-element.108), channel_id=1, source_target_pairs={{0,1},{1,2},{2,3},{3,0},{4,5},{5,6},{6,7},{7,4},{8,9},{9,10},{10,1... | collective-permute-start | bytes 712712 | tf_op jit(solution)/shard_map/ppermute | solution.py:22
  84.9 13.0 %collective-permute-start.7 = (f32[2,58,2,256]{3,1,2,0:T(8,128)S(1)}, f32[2,58,2,256]{3,1,2,0:T(8,128)S(1)}, u32[]{:S(2)}, u32[]{:S(2)}) collective-permute-start(f32[2,58,2,256]{3,1,2,0:T(8,128)S(1)} %get-tuple-element.107), channel_id=1, source_target_pairs={{1,0},{2,1},{3,2},{0,3},{5,4},{6,5},{7,6},{4,7},{9,8},{10,9},{11,1... | collective-permute-start | bytes 712712 | tf_op jit(solution)/shard_map/ppermute | solution.py:23
  141.0 9.5 %all-to-all-start.2 = ((f32[8,34,116]{2,1,0:T(8,128)}), f32[8,34,116]{2,1,0:T(8,128)S(1)}, u32[]{:S(2)}, u32[]{:S(2)}) async-start(f32[8,34,116]{2,1,0:T(8,128)} %reshape.78), calls=%async_computation.2 | async-start | bytes 327680 | tf_op jit(solution)/shard_map/all_to_all | solution.py:110
Sparse Core Ops, SparseCore 0:
  104.6 33.4 all-reduce.3
where the time goes:
time: 159 us
  waiting for transfers between devices  68.8 us (43%)
  starting transfers between devices  28.6 us (18%)
  other arithmetic  28 us (18%)
  local copies, waits for them, and re-layouts  18.8 us (12%)
  between operations  14.7 us (9%)
    psum x1, waiting for transfers between devices, on_device(): totals = lax.psum(partial_value, 'grp')  33.6 us
    ppermute x4, waiting for transfers between devices, padded(): before = lax.ppermute(last, axis, up)  19.6 us
    add x8, other arithmetic, advance(): centre + courant_here * ((western - eastern) * 0.5)  14.8 us
    ppermute x4, starting transfers between devices, padded(): after = lax.ppermute(leading, axis, down)  11.3 us
    ppermute x4, waiting for transfers between devices, padded(): after = lax.ppermute(leading, axis, down)  8.52 us
    unnamed x20, local copies, waits for them, and re-layouts  6.61 us
    all_to_all x1, starting transfers between devices, on_device(): lax.all_to_all(out_cour, 'col', split_axis=0, concat_axis=0, tiled=True)  5.2 us
    ppermute x4, starting transfers between devices, padded(): before = lax.ppermute(last, axis, up)  4.24 us
  transfers between devices with their start and end apart: 12, of which 9 were waited for; matrix products, arithmetic and copies ran while one was open for 8% of the time, Pallas kernels for 0%

commit v1 on v0

--- a/solution.py
+++ b/solution.py
@@ -101,7 +101,7 @@
         crm_now = advance(middle, courant_here, forcing, cloudy)
     cells_all = crm_state.shape[2] * lax.axis_size("grp")
     partial_value = jnp.sum(crm_now, axis=2) - jnp.sum(crm_state, axis=2)
-    totals = lax.psum(partial_value, "grp")
+    totals = jnp.sum(lax.all_gather(partial_value, "grp"), axis=0)
     increment = totals / cells_all
     phys_inc = increment.transpose(2, 0, 1).reshape(columns, 2 * levels)
     back_rows = (

time: 159 us -> 126 us (0.79)
  waiting for transfers between devices: 68.8 us -> 35.1 us
  blocking collectives: 0 us -> 15.9 us
  between operations: 14.7 us -> 1.3 us
  other arithmetic: 28 us -> 26.4 us
    psum x1 -> x0, waiting for transfers between devices: 33.6 us -> none  [on_device(): totals = lax.psum(partial_value, 'grp')]
    all_gather x0 -> x1, blocking collectives: none -> 15.9 us  [on_device(): totals = jnp.sum(lax.all_gather(partial_value, 'grp'), axis=0)]
  transfers between devices with their start and end apart: 12 -> 11, of which waited for: 9 -> 8; matrix products, arithmetic and copies ran while one was open for 8% -> 10% of each run, Pallas kernels for 0% -> 0%
where the time goes in v1:
time: 126 us
  waiting for transfers between devices  35.1 us (28%)
  starting transfers between devices  28.3 us (22%)
  other arithmetic  26.4 us (21%)
  local copies, waits for them, and re-layouts  18.8 us (15%)
  blocking collectives  15.9 us (13%)
  between operations  1.3 us (1%)
    ppermute x4, waiting for transfers between devices, padded(): before = lax.ppermute(last, axis, up)  19.6 us
    all_gather x1, blocking collectives, on_device(): totals = jnp.sum(lax.all_gather(partial_value, 'grp'), axis=0)  15.9 us
    add x8, other arithmetic, advance(): centre + courant_here * ((western - eastern) * 0.5)  14.8 us
    ppermute x4, starting transfers between devices, padded(): after = lax.ppermute(leading, axis, down)  11.3 us
    ppermute x4, waiting for transfers between devices, padded(): after = lax.ppermute(leading, axis, down)  8.52 us
    unnamed x20, local copies, waits for them, and re-layouts  6.61 us
    all_to_all x1, starting transfers between devices, on_device(): lax.all_to_all(out_cour, 'col', split_axis=0, concat_axis=0, tiled=True)  5.2 us
    ppermute x4, starting transfers between devices, padded(): before = lax.ppermute(last, axis, up)  4.24 us
  transfers between devices with their start and end apart: 11, of which 8 were waited for; matrix products, arithmetic and copies ran while one was open for 10% of the time, Pallas kernels for 0%

profile of v1, /device:TPU:0, one launch (start us, length us, event | category | flops | bytes accessed | tf_op | source)
XLA Modules:
  0.0 125.9 jit_solution(2607312403916868964)
XLA Ops:
  0.7 0.9 and_select_fusion.1
  1.7 0.8 compare_select_fusion.2
  2.5 1.4 %scatter_custom_fusion = s32[272]{0:T(512)S(1)} fusion(s32[256]{0:T(256)S(1)} %compare_select_fusion.2, s32[256]{0:T(256)S(1)} %iota.32, s32[]{:T(128)} %constant.48.clone.1), kind=kCustom, calls=%fused_computation.268 | custom fusion | bytes 1092 | tf_op jit(solution)/shard_map/scatter | solution.py:65
  4.0 0.9 copy.71
  4.9 1.1 gather_fusion
  6.0 0.9 reshape.161
  6.9 5.2 %all-to-all-start = ((f32[8,1,1972]{2,1,0:T(1,128)}), f32[8,1,1972]{2,1,0:T(1,128)S(1)}, u32[]{:S(2)}, u32[]{:S(2)}) async-start(f32[8,1,1972]{2,1,0:T(1,128)} %reshape.161), calls=%async_computation | async-start | bytes 131072 | tf_op jit(solution)/shard_map/all_to_all | solution.py:72
  12.3 1.6 %collective-permute-start = (f32[2,58,2,256]{3,1,2,0:T(8,128)S(1)}, f32[2,58,2,256]{3,1,2,0:T(8,128)S(1)}, u32[]{:S(2)}, u32[]{:S(2)}) collective-permute-start(f32[2,58,2,256]{3,1,2,0:T(8,128)S(1)} %copy.84), channel_id=1, source_target_pairs={{0,1},{1,2},{2,3},{3,0},{4,5},{5,6},{6,7},{7,4},{8,9},{9,10},{10,1... | collective-permute-start | bytes 712712 | tf_op jit(solution)/shard_map/ppermute | solution.py:22
  13.9 2.3 %collective-permute-start.1 = (f32[2,58,2,256]{3,1,2,0:T(8,128)S(1)}, f32[2,58,2,256]{3,1,2,0:T(8,128)S(1)}, u32[]{:S(2)}, u32[]{:S(2)}) collective-permute-start(f32[2,58,2,256]{3,1,2,0:T(8,128)S(1)} %copy.85), channel_id=1, source_target_pairs={{1,0},{2,1},{3,2},{0,3},{5,4},{6,5},{7,6},{4,7},{9,8},{10,9},{11,1... | collective-permute-start | bytes 712712 | tf_op jit(solution)/shard_map/ppermute | solution.py:23
  16.3 0.6 reduce-window.6
  17.4 0.5 while.11
  18.1 1.1 gather_fusion.2
  19.1 0.7 reshape.87
  19.8 4.2 %all-to-all-start.1 = ((f32[8,34,116]{2,1,0:T(8,128)}), f32[8,34,116]{2,1,0:T(8,128)S(1)}, u32[]{:S(2)}, u32[]{:S(2)}) async-start(f32[8,34,116]{2,1,0:T(8,128)} %reshape.87), calls=%async_computation.1 | async-start | bytes 327680 | tf_op jit(solution)/shard_map/all_to_all | solution.py:71
  24.0 0.5 broadcast.480
  24.5 0.8 reduce.2
  25.4 0.7 gather_fusion.1
  26.3 3.6 %all-to-all-done.1 = f32[8,34,116]{2,1,0:T(8,128)S(1)} async-done(((f32[8,34,116]{2,1,0:T(8,128)}), f32[8,34,116]{2,1,0:T(8,128)S(1)}, u32[]{:S(2)}, u32[]{:S(2)}) %all-to-all-start.1) | async-done | bytes 126240 | tf_op jit(solution)/shard_map/all_to_all | solution.py:71
  29.8 0.7 gather_fusion.3
  30.8 1.3 %constant_dynamic-update-slice_fusion.6 = (f32[2,58,18,256]{3,1,2,0:T(8,128)S(1)}, f32[2,58,20,256]{3,1,2,0:T(8,128)S(1)}, f32[2,58,18,256]{3,1,2,0:T(8,128)S(1)}) fusion(f32[2,58,16,256]{3,2,1,0:T(8,128)S(1)} %copy-done, f32[2,58,20,256]{3,1,2,0:T(8,128)S(1)} %get-tuple-element.121, f32[2,58,18,256]{3,1,2,0:T(8,128)S(1)} %get-tuple-element.120), kind=kLoop, calls=%fused_computation.240 | loop fusion | bytes 8192000
  32.2 0.6 fusion.111
  32.9 1.8 %fusion.44 = f32[2,58,18,256]{3,1,2,0:T(8,128)S(1)} fusion(f32[2,1,18,256]{3,1,2,0:T(1,128)S(1)} %get-tuple-element.78, f32[2,57,18,256]{3,1,2,0:T(8,128)S(1)} %get-tuple-element.80, f32[2,57,18,256]{3,1,2,0:T(8,128)S(1)} %get-tuple-element.79, f32[2,1,18,256]{3,1,2,0:T(1,128)S(1)} %get-tuple-element.77, f32[2,58,18,256]{3,1,2,0:T(8,128)S(1)} %get-tuple-element.115, ...), kind=kLoop, calls=%fused_computation.133 | loop fusion | flops 8017920 | bytes 13006848 | tf_op jit(solution)/shard_map/add | solution.py:43
  34.7 0.5 multiply_add_fusion.3
  35.4 1.7 %fusion.80 = f32[2,58,16,256]{3,1,2,0:T(8,128)S(1)} fusion(f32[1,58,18,256]{3,1,2,0:T(8,128)S(1)} %get-tuple-element.88, f32[1,58,18,256]{3,1,2,0:T(8,128)S(1)} %get-tuple-element.87, f32[2,1,16,256]{3,1,2,0:T(1,128)S(1)} %get-tuple-element.96, f32[2,57,16,256]{3,1,2,0:T(8,128)S(1)} %fusion.60, f32[2,1,16,256]{3,1,2,0:T(1,128)S(1)} %get-tuple-element.95, ...), kind=kLoop, calls=%fused_computation.179 | loop fusion | flops 9027584 | bytes 6150144 | tf_op jit(solution)/shard_map/add | solution.py:43
  37.1 0.5 fusion.88
  37.7 3.8 %collective-permute-start.3 = (f32[2,58,2,256]{3,1,2,0:T(8,128)S(1)}, f32[2,58,2,256]{3,1,2,0:T(8,128)S(1)}, u32[]{:S(2)}, u32[]{:S(2)}) collective-permute-start(f32[2,58,2,256]{3,1,2,0:T(8,128)S(1)} %get-tuple-element.111), channel_id=1, source_target_pairs={{1,0},{2,1},{3,2},{0,3},{5,4},{6,5},{7,6},{4,7},{9,8},{10,9},{11,1... | collective-permute-start | bytes 712712 | tf_op jit(solution)/shard_map/ppermute | solution.py:23
  41.5 7.2 %collective-permute-done.2 = f32[2,58,2,256]{3,1,2,0:T(8,128)S(1)} collective-permute-done((f32[2,58,2,256]{3,1,2,0:T(8,128)S(1)}, f32[2,58,2,256]{3,1,2,0:T(8,128)S(1)}, u32[]{:S(2)}, u32[]{:S(2)}) %collective-permute-start.2) | collective-permute-done | bytes 237600 | tf_op jit(solution)/shard_map/ppermute | solution.py:22
  48.7 2.6 %collective-permute-done.3 = f32[2,58,2,256]{3,1,2,0:T(8,128)S(1)} collective-permute-done((f32[2,58,2,256]{3,1,2,0:T(8,128)S(1)}, f32[2,58,2,256]{3,1,2,0:T(8,128)S(1)}, u32[]{:S(2)}, u32[]{:S(2)}) %collective-permute-start.3) | collective-permute-done | bytes 237600 | tf_op jit(solution)/shard_map/ppermute | solution.py:23
  51.3 0.3 pad_maximum_fusion
  51.6 0.6 fusion.109
  52.2 2.2 %fusion.10 = f32[2,58,18,256]{3,1,2,0:T(8,128)S(1)} fusion(f32[1,58,16,256]{3,1,2,0:T(8,128)S(1)} %get-tuple-element.104, f32[1,58,16,256]{3,1,2,0:T(8,128)S(1)} %get-tuple-element.103, f32[2,58,2,256]{3,1,2,0:T(8,128)S(1)} %collective-permute-done.2, f32[2,58,2,256]{3,1,2,0:T(8,128)S(1)} %collective-permute-done.3, ...), kind=kLoop, calls=%fused_computation.96 | loop fusion | flops 18708480 | bytes 11032576 | tf_op jit(solution)/shard_map/add | solution.py:43
  54.4 0.5 multiply_add_fusion.2
  54.9 0.2 fusion.56
  55.2 1.7 %fusion.75 = f32[2,58,16,256]{3,1,2,0:T(8,128)S(1)} fusion(f32[1,58,18,256]{3,1,2,0:T(8,128)S(1)} %get-tuple-element.86, f32[1,58,18,256]{3,1,2,0:T(8,128)S(1)} %get-tuple-element.85, f32[2,1,16,256]{3,1,2,0:T(1,128)S(1)} %get-tuple-element.94, f32[2,57,16,256]{3,1,2,0:T(8,128)S(1)} %fusion.56, f32[2,1,16,256]{3,1,2,0:T(1,128)S(1)} %get-tuple-element.93, ...), kind=kLoop, calls=%fused_computation.173 | loop fusion | flops 9027584 | bytes 6150144 | tf_op jit(solution)/shard_map/add | solution.py:43
  56.9 0.5 fusion.87
  57.4 0.9 collective-permute-start.4
  58.3 3.0 %collective-permute-start.5 = (f32[2,58,2,256]{3,1,2,0:T(8,128)S(1)}, f32[2,58,2,256]{3,1,2,0:T(8,128)S(1)}, u32[]{:S(2)}, u32[]{:S(2)}) collective-permute-start(f32[2,58,2,256]{3,1,2,0:T(8,128)S(1)} %get-tuple-element.109), channel_id=1, source_target_pairs={{1,0},{2,1},{3,2},{0,3},{5,4},{6,5},{7,6},{4,7},{9,8},{10,9},{11,1... | collective-permute-start | bytes 712712 | tf_op jit(solution)/shard_map/ppermute | solution.py:23
  61.3 7.2 %collective-permute-done.4 = f32[2,58,2,256]{3,1,2,0:T(8,128)S(1)} collective-permute-done((f32[2,58,2,256]{3,1,2,0:T(8,128)S(1)}, f32[2,58,2,256]{3,1,2,0:T(8,128)S(1)}, u32[]{:S(2)}, u32[]{:S(2)}) %collective-permute-start.4) | collective-permute-done | bytes 237600 | tf_op jit(solution)/shard_map/ppermute | solution.py:22
  68.4 2.3 %collective-permute-done.5 = f32[2,58,2,256]{3,1,2,0:T(8,128)S(1)} collective-permute-done((f32[2,58,2,256]{3,1,2,0:T(8,128)S(1)}, f32[2,58,2,256]{3,1,2,0:T(8,128)S(1)}, u32[]{:S(2)}, u32[]{:S(2)}) %collective-permute-start.5) | collective-permute-done | bytes 237600 | tf_op jit(solution)/shard_map/ppermute | solution.py:23
  70.7 0.3 pad_maximum_fusion.1
  71.0 0.6 fusion.108
  71.6 2.2 %fusion.23 = f32[2,58,18,256]{3,1,2,0:T(8,128)S(1)} fusion(f32[1,58,16,256]{3,1,2,0:T(8,128)S(1)} %get-tuple-element.102, f32[1,58,16,256]{3,1,2,0:T(8,128)S(1)} %get-tuple-element.101, f32[2,58,2,256]{3,1,2,0:T(8,128)S(1)} %collective-permute-done.4, f32[2,58,2,256]{3,1,2,0:T(8,128)S(1)} %collective-permute-done.5, ...), kind=kLoop, calls=%fused_computation.109 | loop fusion | flops 18708480 | bytes 11032576 | tf_op jit(solution)/shard_map/add | solution.py:43
  73.8 0.5 multiply_add_fusion.1
  74.3 0.2 fusion.52
  74.6 1.7 %fusion.70 = f32[2,58,16,256]{3,1,2,0:T(8,128)S(1)} fusion(f32[1,58,18,256]{3,1,2,0:T(8,128)S(1)} %get-tuple-element.84, f32[1,58,18,256]{3,1,2,0:T(8,128)S(1)} %get-tuple-element.83, f32[2,1,16,256]{3,1,2,0:T(1,128)S(1)} %get-tuple-element.92, f32[2,57,16,256]{3,1,2,0:T(8,128)S(1)} %fusion.52, f32[2,1,16,256]{3,1,2,0:T(1,128)S(1)} %get-tuple-element.91, ...), kind=kLoop, calls=%fused_computation.167 | loop fusion | flops 9027584 | bytes 6150144 | tf_op jit(solution)/shard_map/add | solution.py:43
  76.2 0.4 fusion.86
  76.7 1.7 %collective-permute-start.6 = (f32[2,58,2,256]{3,1,2,0:T(8,128)S(1)}, f32[2,58,2,256]{3,1,2,0:T(8,128)S(1)}, u32[]{:S(2)}, u32[]{:S(2)}) collective-permute-start(f32[2,58,2,256]{3,1,2,0:T(8,128)S(1)} %get-tuple-element.108), channel_id=1, source_target_pairs={{0,1},{1,2},{2,3},{3,0},{4,5},{5,6},{6,7},{7,4},{8,9},{9,10},{10,1... | collective-permute-start | bytes 712712 | tf_op jit(solution)/shard_map/ppermute | solution.py:22
  78.4 2.2 %collective-permute-start.7 = (f32[2,58,2,256]{3,1,2,0:T(8,128)S(1)}, f32[2,58,2,256]{3,1,2,0:T(8,128)S(1)}, u32[]{:S(2)}, u32[]{:S(2)}) collective-permute-start(f32[2,58,2,256]{3,1,2,0:T(8,128)S(1)} %get-tuple-element.107), channel_id=1, source_target_pairs={{1,0},{2,1},{3,2},{0,3},{5,4},{6,5},{7,6},{4,7},{9,8},{10,9},{11,1... | collective-permute-start | bytes 712712 | tf_op jit(solution)/shard_map/ppermute | solution.py:23
  80.6 1.9 %reduce_sum.47 = f32[2,58,256]{2,1,0:T(8,128)S(1)} reduce(f32[2,58,16,256]{3,2,1,0:T(8,128)} %param.11, f32[]{:T(128)} %constant.35.clone.1), dimensions={2}, to_apply=%region_8.9 | reduce | flops 445440 | bytes 2019332 | tf_op jit(solution)/shard_map/reduce_sum | solution.py:103
  82.4 5.3 %collective-permute-done.6 = f32[2,58,2,256]{3,1,2,0:T(8,128)S(1)} collective-permute-done((f32[2,58,2,256]{3,1,2,0:T(8,128)S(1)}, f32[2,58,2,256]{3,1,2,0:T(8,128)S(1)}, u32[]{:S(2)}, u32[]{:S(2)}) %collective-permute-start.6) | collective-permute-done | bytes 237600 | tf_op jit(solution)/shard_map/ppermute | solution.py:22
  87.8 3.6 %collective-permute-done.7 = f32[2,58,2,256]{3,1,2,0:T(8,128)S(1)} collective-permute-done((f32[2,58,2,256]{3,1,2,0:T(8,128)S(1)}, f32[2,58,2,256]{3,1,2,0:T(8,128)S(1)}, u32[]{:S(2)}, u32[]{:S(2)}) %collective-permute-start.7) | collective-permute-done | bytes 237600 | tf_op jit(solution)/shard_map/ppermute | solution.py:23
  91.5 0.6 fusion.107
  92.2 2.0 %fusion.36 = f32[2,58,18,256]{3,1,2,0:T(8,128)S(1)} fusion(f32[1,58,16,256]{3,1,2,0:T(8,128)S(1)} %get-tuple-element.100, f32[1,58,16,256]{3,1,2,0:T(8,128)S(1)} %get-tuple-element.99, f32[2,58,2,256]{3,1,2,0:T(8,128)S(1)} %collective-permute-done.6, f32[2,58,2,256]{3,1,2,0:T(8,128)S(1)} %collective-permute-done.7, ...), kind=kLoop, calls=%fused_computation.122 | loop fusion | flops 18708480 | bytes 11032576 | tf_op jit(solution)/shard_map/add | solution.py:43
  94.2 0.5 multiply_add_fusion
  95.0 1.7 %fusion.65 = f32[2,58,16,256]{3,1,2,0:T(8,128)S(1)} fusion(f32[1,58,18,256]{3,1,2,0:T(8,128)S(1)} %get-tuple-element.82, f32[1,58,18,256]{3,1,2,0:T(8,128)S(1)} %get-tuple-element.81, f32[2,1,16,256]{3,1,2,0:T(1,128)S(1)} %get-tuple-element.90, f32[2,57,16,256]{3,1,2,0:T(8,128)S(1)} %fusion.48, f32[2,1,16,256]{3,1,2,0:T(1,128)S(1)} %get-tuple-element.89, ...), kind=kLoop, calls=%fused_computation.161 | loop fusion | flops 9027584 | bytes 6150144 | tf_op jit(solution)/shard_map/add | solution.py:43
  96.7 0.4 multiply_add_fusion.4
  97.3 15.9 %all-gather = f32[8,58,256]{2,1,0:T(8,128)S(1)} all-gather(f32[2,58,256]{2,1,0:T(8,128)S(1)} %sub.260), channel_id=2, replica_groups=mesh['col'=8,'grp'=4] {'grp'}, dimensions={0}, use_global_device_ids=true | all-gather | bytes 593920 | tf_op jit(solution)/shard_map/all_gather | solution.py:104
  113.4 1.2 scatter_custom_fusion.1
  114.5 0.7 reshape.90
  115.2 3.4 %all-to-all-start.2 = ((f32[8,34,116]{2,1,0:T(8,128)}), f32[8,34,116]{2,1,0:T(8,128)S(1)}, u32[]{:S(2)}, u32[]{:S(2)}) async-start(f32[8,34,116]{2,1,0:T(8,128)} %reshape.90), calls=%async_computation.2 | async-start | bytes 327680 | tf_op jit(solution)/shard_map/all_to_all | solution.py:110
  118.6 2.4 %copy.78 = f32[2,58,16,256]{3,2,1,0:T(8,128)} copy(f32[2,58,16,256]{3,1,2,0:T(8,128)S(1)} %get-tuple-element.105) | data formatting | bytes 3801088
  121.0 3.4 %all-to-all-done.2 = f32[8,34,116]{2,1,0:T(8,128)S(1)} async-done(((f32[8,34,116]{2,1,0:T(8,128)}), f32[8,34,116]{2,1,0:T(8,128)S(1)}, u32[]{:S(2)}, u32[]{:S(2)}) %all-to-all-start.2) | async-done | bytes 126240 | tf_op jit(solution)/shard_map/all_to_all | solution.py:110
  124.4 0.7 gather_fusion.4
  125.1 0.8 copy.77
  (75 shorter events, 3.4 us)
Async XLA Ops:
  0.6 15.6 %copy-start.2 = (s32[2048]{0:T(1024)S(1)}, s32[2048]{0:T(1024)}, u32[]{:S(2)}) copy-start(s32[2048]{0:T(1024)} %param.9) | copy-start | bytes 24580
  0.6 11.4 %copy-start = (f32[2,58,16,256]{3,2,1,0:T(8,128)S(1)}, f32[2,58,16,256]{3,2,1,0:T(8,128)}, u32[]{:S(2)}) copy-start(f32[2,58,16,256]{3,2,1,0:T(8,128)} %param.11) | copy-start | bytes 5701636
  4.9 13.0 %copy-start.3 = (s32[256]{0:T(256)S(1)}, s32[256]{0:T(256)}, u32[]{:S(2)}) copy-start(s32[256]{0:T(256)} %param.10) | copy-start | bytes 3076
  4.9 13.0 %copy-start.1 = (f32[256,116]{0,1:T(8,128)S(1)}, f32[256,116]{0,1:T(8,128)}, u32[]{:S(2)}) copy-start(f32[256,116]{0,1:T(8,128)} %param.7) | copy-start | bytes 356356
  6.9 12.9 %all-to-all-start = ((f32[8,1,1972]{2,1,0:T(1,128)}), f32[8,1,1972]{2,1,0:T(1,128)S(1)}, u32[]{:S(2)}, u32[]{:S(2)}) async-start(f32[8,1,1972]{2,1,0:T(1,128)} %reshape.161), calls=%async_computation | async-start | bytes 131072 | tf_op jit(solution)/shard_map/all_to_all | solution.py:72
  12.3 18.4 %collective-permute-start = (f32[2,58,2,256]{3,1,2,0:T(8,128)S(1)}, f32[2,58,2,256]{3,1,2,0:T(8,128)S(1)}, u32[]{:S(2)}, u32[]{:S(2)}) collective-permute-start(f32[2,58,2,256]{3,1,2,0:T(8,128)S(1)} %copy.84), channel_id=1, source_target_pairs={{0,1},{1,2},{2,3},{3,0},{4,5},{5,6},{6,7},{7,4},{8,9},{9,10},{10,1... | collective-permute-start | bytes 712712 | tf_op jit(solution)/shard_map/ppermute | solution.py:22
  13.9 18.2 %collective-permute-start.1 = (f32[2,58,2,256]{3,1,2,0:T(8,128)S(1)}, f32[2,58,2,256]{3,1,2,0:T(8,128)S(1)}, u32[]{:S(2)}, u32[]{:S(2)}) collective-permute-start(f32[2,58,2,256]{3,1,2,0:T(8,128)S(1)} %copy.85), channel_id=1, source_target_pairs={{1,0},{2,1},{3,2},{0,3},{5,4},{6,5},{7,6},{4,7},{9,8},{10,9},{11,1... | collective-permute-start | bytes 712712 | tf_op jit(solution)/shard_map/ppermute | solution.py:23
  19.8 10.0 %all-to-all-start.1 = ((f32[8,34,116]{2,1,0:T(8,128)}), f32[8,34,116]{2,1,0:T(8,128)S(1)}, u32[]{:S(2)}, u32[]{:S(2)}) async-start(f32[8,34,116]{2,1,0:T(8,128)} %reshape.87), calls=%async_computation.1 | async-start | bytes 327680 | tf_op jit(solution)/shard_map/all_to_all | solution.py:71
  37.7 11.0 %collective-permute-start.2 = (f32[2,58,2,256]{3,1,2,0:T(8,128)S(1)}, f32[2,58,2,256]{3,1,2,0:T(8,128)S(1)}, u32[]{:S(2)}, u32[]{:S(2)}) collective-permute-start(f32[2,58,2,256]{3,1,2,0:T(8,128)S(1)} %get-tuple-element.112), channel_id=1, source_target_pairs={{0,1},{1,2},{2,3},{3,0},{4,5},{5,6},{6,7},{7,4},{8,9},{9,10},{10,1... | collective-permute-start | bytes 712712 | tf_op jit(solution)/shard_map/ppermute | solution.py:22
  37.7 13.6 %collective-permute-start.3 = (f32[2,58,2,256]{3,1,2,0:T(8,128)S(1)}, f32[2,58,2,256]{3,1,2,0:T(8,128)S(1)}, u32[]{:S(2)}, u32[]{:S(2)}) collective-permute-start(f32[2,58,2,256]{3,1,2,0:T(8,128)S(1)} %get-tuple-element.111), channel_id=1, source_target_pairs={{1,0},{2,1},{3,2},{0,3},{5,4},{6,5},{7,6},{4,7},{9,8},{10,9},{11,1... | collective-permute-start | bytes 712712 | tf_op jit(solution)/shard_map/ppermute | solution.py:23
  57.4 11.0 %collective-permute-start.4 = (f32[2,58,2,256]{3,1,2,0:T(8,128)S(1)}, f32[2,58,2,256]{3,1,2,0:T(8,128)S(1)}, u32[]{:S(2)}, u32[]{:S(2)}) collective-permute-start(f32[2,58,2,256]{3,1,2,0:T(8,128)S(1)} %get-tuple-element.110), channel_id=1, source_target_pairs={{0,1},{1,2},{2,3},{3,0},{4,5},{5,6},{6,7},{7,4},{8,9},{9,10},{10,1... | collective-permute-start | bytes 712712 | tf_op jit(solution)/shard_map/ppermute | solution.py:22
  58.3 12.4 %collective-permute-start.5 = (f32[2,58,2,256]{3,1,2,0:T(8,128)S(1)}, f32[2,58,2,256]{3,1,2,0:T(8,128)S(1)}, u32[]{:S(2)}, u32[]{:S(2)}) collective-permute-start(f32[2,58,2,256]{3,1,2,0:T(8,128)S(1)} %get-tuple-element.109), channel_id=1, source_target_pairs={{1,0},{2,1},{3,2},{0,3},{5,4},{6,5},{7,6},{4,7},{9,8},{10,9},{11,1... | collective-permute-start | bytes 712712 | tf_op jit(solution)/shard_map/ppermute | solution.py:23
  76.7 11.1 %collective-permute-start.6 = (f32[2,58,2,256]{3,1,2,0:T(8,128)S(1)}, f32[2,58,2,256]{3,1,2,0:T(8,128)S(1)}, u32[]{:S(2)}, u32[]{:S(2)}) collective-permute-start(f32[2,58,2,256]{3,1,2,0:T(8,128)S(1)} %get-tuple-element.108), channel_id=1, source_target_pairs={{0,1},{1,2},{2,3},{3,0},{4,5},{5,6},{6,7},{7,4},{8,9},{9,10},{10,1... | collective-permute-start | bytes 712712 | tf_op jit(solution)/shard_map/ppermute | solution.py:22
  78.4 13.0 %collective-permute-start.7 = (f32[2,58,2,256]{3,1,2,0:T(8,128)S(1)}, f32[2,58,2,256]{3,1,2,0:T(8,128)S(1)}, u32[]{:S(2)}, u32[]{:S(2)}) collective-permute-start(f32[2,58,2,256]{3,1,2,0:T(8,128)S(1)} %get-tuple-element.107), channel_id=1, source_target_pairs={{1,0},{2,1},{3,2},{0,3},{5,4},{6,5},{7,6},{4,7},{9,8},{10,9},{11,1... | collective-permute-start | bytes 712712 | tf_op jit(solution)/shard_map/ppermute | solution.py:23
  115.2 9.2 %all-to-all-start.2 = ((f32[8,34,116]{2,1,0:T(8,128)}), f32[8,34,116]{2,1,0:T(8,128)S(1)}, u32[]{:S(2)}, u32[]{:S(2)}) async-start(f32[8,34,116]{2,1,0:T(8,128)} %reshape.90), calls=%async_computation.2 | async-start | bytes 327680 | tf_op jit(solution)/shard_map/all_to_all | solution.py:110
